TPU v7x, 32 devices: a whole 2x2x4 slice. The times are simulated.
32 devices in a mesh: ao: 8 (over y, x, core), aux: 4 (over z).
Axes of the slice: x: 2, y: 2, z: 4, core: 2. Of those that a mesh axis runs over, the one named last changes fastest.
Arguments:
- blocks: bfloat16 [48, 256, 128, 128], P('ao', 'aux'), may hold values from -6 to 6
- pairs: int32 [48, 2], P('ao'), may hold values from 0 to 79, as said below
- counts: int32 [8], P('ao'), may hold values from 1 to 6, as said below
- owned_blocks: int32 [80], P('ao'), may hold values from 0 to 79, as said below
- occ_coef: bfloat16 [80, 8, 128], P('ao'), may hold values from -0.5 to 0.5
- vir_coef: bfloat16 [10240, 9216], P('ao', 'aux'), may hold values from -0.109375 to 0.109375
Outputs:
- b_tensor: bfloat16 [256, 8, 9216], P('ao', None, 'aux')
Inputs may be any that keep to these rules, and one draw needn't show every extreme that they name: `pairs`: among the used slots of one ao index, at most 3 have nu blocks whose rows one owner holds; in every draw some index reaches 3. `counts`: some ao index uses all 6 slots in every draw. `owned_blocks`: every atom block appears exactly once.
All inputs are finite; a program needn't handle non-finite values.
Results may differ from a plain program's by a relative error of at most 0.014.
Values may be sent and summed in bfloat16 or wider, within the bound.
A program may use at most 128 MiB of HBM per device.

v0:
```python
import jax
import jax.numpy as jnp
from jax import lax
from jax.sharding import PartitionSpec as P


def block_place(block_ids, owned_all):
    hits = block_ids[..., None] == owned_all
    positions = jnp.arange(owned_all.shape[0], dtype=jnp.int32)
    return jnp.sum(jnp.where(hits, positions, 0), axis=-1)


def per_device(blocks, pairs, counts, owned_blocks, occ_coef, vir_coef):
    groups = lax.axis_size("ao")
    own_index = lax.axis_index("ao")
    slot_count = blocks.shape[0]
    aux_depth = blocks.shape[1]
    block_width = blocks.shape[3]
    occupied = occ_coef.shape[1]
    all_pairs, all_counts, all_owned = (
        lax.all_gather(pairs, "ao", axis=0, tiled=True),
        lax.all_gather(counts, "ao", axis=0, tiled=True),
        lax.all_gather(owned_blocks, "ao", axis=0, tiled=True),
    )
    occ_all = lax.all_gather(occ_coef, "ao", axis=0, tiled=True)
    total_blocks = all_owned.shape[0]
    per_owner = total_blocks // groups
    slot_ids = jnp.arange(slot_count, dtype=jnp.int32)
    in_use = slot_ids < counts[0]
    occ_pick = occ_all[block_place(pairs[:, 0], all_owned)]
    slab_values = jnp.einsum("sim,spmn->spin", occ_pick, blocks, preferred_element_type=jnp.float32)
    slab_values = jnp.where(in_use[:, None, None, None], slab_values, 0.0).astype(jnp.bfloat16)
    flat_slabs = slab_values.reshape(slot_count, aux_depth * occupied, block_width)
    place_all = block_place(all_pairs[:, 1], all_owned).reshape(groups, slot_count)
    owner_all = place_all // per_owner
    local_all = place_all % per_owner
    live_all = slot_ids[None, :] < all_counts[:, None]
    mine_all = live_all & (owner_all == own_index)
    local_ids = jnp.arange(per_owner, dtype=jnp.int32)
    slabs_got = lax.all_gather(flat_slabs, "ao", axis=0, tiled=True)
    assign = (
        mine_all.reshape(-1)[None, :] & (local_all.reshape(-1)[None, :] == local_ids[:, None])
    ).astype(jnp.bfloat16)
    summed = jnp.einsum("lt,tqm->qlm", assign, slabs_got, preferred_element_type=jnp.float32)
    rows_local = summed.reshape(summed.shape[0], per_owner * block_width).astype(jnp.bfloat16)
    rows_whole = lax.all_gather(rows_local, "aux", axis=0, tiled=True)
    share = rows_whole.shape[0] // groups
    result = lax.psum_scatter(
        jnp.dot(rows_whole, vir_coef, preferred_element_type=jnp.float32).astype(jnp.bfloat16),
        "ao",
        scatter_dimension=0,
        tiled=True,
    ).astype(jnp.float32)
    return result.reshape(share // occupied, occupied, vir_coef.shape[1]).astype(jnp.bfloat16)


def solution(mesh):
    in_specs = (
        P("ao", "aux", None, None),
        P("ao", None),
        P("ao"),
        P("ao"),
        P("ao", None, None),
        P("ao", "aux"),
    )
    out_specs = P("ao", None, "aux")
    return jax.shard_map(
        per_device, mesh=mesh, in_specs=in_specs, out_specs=out_specs, check_vma=False
    )
```

profile of v0, /device:TPU:0, one launch (start us, length us, event | category | flops | bytes accessed | tf_op | source)
XLA Modules:
  0.0 291.0 jit_solution(9892513670469097050)
XLA Ops:
  6.5 0.0 all-gather.4.cloned.1.call-start
  7.2 0.7 slice_bitcast_fusion.1
  7.9 1.3 dynamic-slice
  9.9 0.8 dynamic-update-slice.1
  10.7 0.8 dynamic-update-slice
  11.5 9.5 %all-reduce.2 = (s32[80]{0:T(128)S(1)}, s32[8]{0:T(128)S(1)}) all-reduce(s32[80]{0:T(128)S(1)} %dynamic-update-slice, s32[8]{0:T(128)S(1)} %dynamic-update-slice.1), channel_id=1, replica_groups=mesh['ao'=8,'aux'=4] {'ao'}, use_global_device_ids=true, to_apply=%add | all-reduce | flops 88 | bytes 704
  21.0 0.2 select_reduce_fusion.1
  21.2 8.6 %all_gather.18 = bf16[80,8,128]{2,1,0:T(8,128)(2,1)S(1)} all-gather(bf16[10,8,128]{2,1,0:T(8,128)(2,1)} %param.10), channel_id=1, replica_groups=mesh['ao'=8,'aux'=4] {'ao'}, dimensions={0}, use_global_device_ids=true | all-gather | bytes 184320 | tf_op jit(solution)/shard_map/all_gather | solution.py:25
  29.8 0.6 gather_fusion
  30.4 0.0 copy-start
  30.4 7.2 %fusion.4 = bf16[6,512,128]{2,1,0:T(8,128)(2,1)} fusion(bf16[6,64,128,128]{3,2,1,0:T(8,128)(2,1)} %param.6, pred[6]{0:T(512)(128)(4,1)S(1)} %iota_compare_fusion.2, bf16[6,8,128]{2,1,0:T(8,128)(2,1)S(1)} %gather_fusion), kind=kOutput, calls=%fused_computation.6 | convolution fusion | flops 101449728 | bytes 13381638 | tf_op jit(solution)/shard_map/sim,spmn->spin/dot_general | solution.py:31
  37.6 0.0 all-gather.4.cloned.1.call-update
  37.6 0.0 all-gather.6.cloned.1.call-start
  37.7 0.1 iota_compare_fusion.1
  37.8 0.1 lt.52
  37.9 0.0 copy-done
  37.9 8.6 %all-gather = s32[8,6,2]{1,2,0:T(2,128)S(1)} all-gather(s32[1,6,2]{1,2,0:T(2,128)S(1)} %bitcast.35), channel_id=1, replica_groups=mesh['ao'=8,'aux'=4] {'ao'}, dimensions={0}, use_global_device_ids=true | all-gather | bytes 432 | tf_op jit(solution)/shard_map/all_gather | solution.py:21
  46.5 0.1 reshape.75
  46.5 0.2 select_reduce_fusion
  46.8 36.7 %all-gather.4.cloned.1.call-done = bf16[48,512,128]{2,1,0:T(8,128)(2,1)} async-done(((bf16[6,512,128]{2,1,0:T(8,128)(2,1)}), bf16[48,512,128]{2,1,0:T(8,128)(2,1)}) %all-gather.4.cloned.1.call-update) | async-done | bytes 6291472 | tf_op jit(solution)/shard_map/all_gather | solution.py:40
  83.5 6.4 %convert_bitcast_fusion = bf16[512,10,128]{2,1,0:T(8,128)(2,1)S(1)} fusion(bf16[48,512,128]{2,1,0:T(8,128)(2,1)} %all-gather.4.cloned.1.call-done, s32[48]{0:T(128)S(1)} %and_select_fusion, pred[48]{0:T(512)(128)(4,1)S(1)} %compare_and_fusion), kind=kOutput, calls=%fused_computation.4 | convolution fusion | flops 63570880 | bytes 7602416 | tf_op jit(solution)/shard_map/lt,tqm->qlm/dot_general | solution.py:44
  89.9 2.6 copy.17
  92.5 0.0 all-gather.6.cloned.1.call-update
  92.5 0.2 reduce-scatter.2.cloned.1.call-start
  92.7 98.0 %all-gather.6.cloned.1.call-done = bf16[2048,1280]{0,1:T(8,128)(2,1)} async-done(((bf16[512,1280]{0,1:T(8,128)(2,1)}), bf16[2048,1280]{0,1:T(8,128)(2,1)}) %all-gather.6.cloned.1.call-update) | async-done | bytes 5242896 | tf_op jit(solution)/shard_map/all_gather | solution.py:46
  190.7 18.4 %convolution_convert_fusion = bf16[2048,2304]{1,0:T(8,128)(2,1)} fusion(bf16[2048,1280]{0,1:T(8,128)(2,1)} %all-gather.6.cloned.1.call-done, bf16[1280,2304]{1,0:T(8,128)(2,1)} %param.11), kind=kOutput, calls=%fused_computation.1 | convolution fusion | flops 12084314112 | bytes 20578304 | tf_op jit(solution)/shard_map/dot_general | solution.py:49
  209.1 0.0 reduce-scatter.2.cloned.1.call-update
  209.1 75.3 %reduce-scatter.2.cloned.1.call-done = bf16[256,2304]{1,0:T(8,128)(2,1)} async-done(((bf16[2048,2304]{1,0:T(8,128)(2,1)}), bf16[256,2304]{1,0:T(8,128)(2,1)}) %reduce-scatter.2.cloned.1.call-update) | async-done | bytes 1179664 | tf_op jit(solution)/shard_map/reduce_scatter | solution.py:48
  (9 shorter events, 0.1 us)
Async XLA Ops:
  6.5 76.9 %all-gather.4.cloned.1.call-start = ((), (), s32[]{:S(2)}) async-start(), calls=%async_computation.1 | async-start | bytes 7077888 | tf_op jit(solution)/shard_map/all_gather | solution.py:40
  30.4 7.5 %copy-start = (s32[6,2]{0,1:T(2,128)S(1)}, s32[6,2]{0,1:T(2,128)}, u32[]{:S(2)}) copy-start(s32[6,2]{0,1:T(2,128)} %param.7) | copy-start | bytes 148
  37.6 153.0 %all-gather.6.cloned.1.call-start = ((), (), s32[]{:S(2)}) async-start(), calls=%async_computation.2 | async-start | bytes 6553600 | tf_op jit(solution)/shard_map/all_gather | solution.py:46
  92.5 191.9 %reduce-scatter.2.cloned.1.call-start = ((), (), s32[]{:S(2)}) async-start(), calls=%async_computation.3 | async-start | bytes 10616832 | tf_op jit(solution)/shard_map/reduce_scatter | solution.py:48
Sparse Core Ops, SparseCore 0:
  37.8 45.6 all-gather.3
  92.6 98.0 all-gather.5
  209.2 75.1 reduce-scatter.1
where the time goes:
time: 291 us
  waiting for transfers between devices  210 us (72%)
  matrix products  32.1 us (11%)
  blocking collectives  26.7 us (9%)
  between operations  14.5 us (5%)
  local copies, waits for them, and re-layouts  6.95 us (2%)
    all_gather x1, waiting for transfers between devices, per_device(): rows_whole = lax.all_gather(rows_local, 'aux', axis=0, tiled=True)  98 us
    reduce_scatter x1, waiting for transfers between devices, per_device(): lax.psum_scatter(jnp.dot(rows_whole, vir_coef, preferred_element_type=jnp...  75.3 us
    all_gather x1, waiting for transfers between devices, per_device(): slabs_got = lax.all_gather(flat_slabs, 'ao', axis=0, tiled=True)  36.7 us
    dot_general x1, matrix products, per_device(): jnp.dot(rows_whole, vir_coef, preferred_element_type=jnp.float32)  18.4 us
    unnamed x1, blocking collectives  9.49 us
    all_gather x1, blocking collectives, per_device(): occ_all = lax.all_gather(occ_coef, 'ao', axis=0, tiled=True)  8.6 us
    all_gather x1, blocking collectives, per_device(): lax.all_gather(pairs, 'ao', axis=0, tiled=True)  8.59 us
    dot_general x1, matrix products, per_device(): jnp.einsum('sim,spmn->spin', occ_pick, blocks, preferred_element_type=jnp...  7.2 us
  transfers between devices with their start and end apart: 3, of which 3 were waited for; matrix products, arithmetic and copies ran while one was open for 0% of the time, Pallas kernels for 0%

commit v1 on v0

--- a/solution.py
+++ b/solution.py
@@ -43,7 +43,21 @@
     ).astype(jnp.bfloat16)
     summed = jnp.einsum("lt,tqm->qlm", assign, slabs_got, preferred_element_type=jnp.float32)
     rows_local = summed.reshape(summed.shape[0], per_owner * block_width).astype(jnp.bfloat16)
-    rows_whole = lax.all_gather(rows_local, "aux", axis=0, tiled=True)
+    ways, here, step = (lax.axis_size("aux"), lax.axis_index("aux"), rows_local.shape[0])
+    shape = [n * ways if d == 0 else n for d, n in enumerate(rows_local.shape)]
+    full = lax.dynamic_update_slice_in_dim(
+        jnp.zeros(shape, rows_local.dtype), rows_local, here * step, axis=0
+    )
+    going_up = going_down = rows_local
+    for far in range(1, ways // 2 + 1):
+        going_up = lax.ppermute(going_up, "aux", [(d, (d + 1) % ways) for d in range(ways)])
+        full = lax.dynamic_update_slice_in_dim(full, going_up, (here - far) % ways * step, axis=0)
+        if 2 * far < ways:
+            going_down = lax.ppermute(going_down, "aux", [(d, (d - 1) % ways) for d in range(ways)])
+            full = lax.dynamic_update_slice_in_dim(
+                full, going_down, (here + far) % ways * step, axis=0
+            )
+    rows_whole = full
     share = rows_whole.shape[0] // groups
     result = lax.psum_scatter(
         jnp.dot(rows_whole, vir_coef, preferred_element_type=jnp.float32).astype(jnp.bfloat16),

time: 291 us -> 279 us (0.959)
  waiting for transfers between devices: 210 us -> 195 us
  starting transfers between devices: 0.27 us -> 3.92 us
  matrix products: 32.1 us -> 28.9 us
    all_gather x1 -> x0, waiting for transfers between devices: 98 us -> none  [per_device(): rows_whole = lax.all_gather(rows_local, 'aux', axis=0, tiled=True)]
    ppermute x0 -> x3, waiting for transfers between devices: none -> 82.7 us  [the longest x2 56.8 us: per_device(): lax.ppermute(going_up, 'aux', [(d, (d + 1) % ways) for d in range(ways)])]
    ppermute x0 -> x3, starting transfers between devices: none -> 3.88 us  [the longest x1 2.34 us: per_device(): lax.ppermute(going_down, 'aux', [(d, (d - 1) % ways) for d in range(ways)])]
    dynamic_update_slice x0 -> x4, local copies, waits for them, and re-layouts: none -> 3.35 us  [the longest x2 1.68 us: per_device(): lax.dynamic_update_slice_in_dim(full, going_up, (here - far) % ways * ste...]
    dot_general x1, matrix products: 18.4 us -> 15.2 us  [per_device(): jnp.dot(rows_whole, vir_coef, preferred_element_type=jnp.float32)]
  transfers between devices with their start and end apart: 3 -> 5, of which waited for: 3 -> 5; matrix products, arithmetic and copies ran while one was open for 0% -> 1% of each run, Pallas kernels for 0% -> 0%
where the time goes in v1:
time: 279 us
  waiting for transfers between devices  195 us (70%)
  matrix products  28.9 us (10%)
  blocking collectives  26.7 us (10%)
  between operations  14.8 us (5%)
  local copies, waits for them, and re-layouts  9.78 us (4%)
  starting transfers between devices  3.92 us (1%)
    reduce_scatter x1, waiting for transfers between devices, per_device(): lax.psum_scatter(jnp.dot(rows_whole, vir_coef, preferred_element_type=jnp...  75.1 us
    ppermute x2, waiting for transfers between devices, per_device(): lax.ppermute(going_up, 'aux', [(d, (d + 1) % ways) for d in range(ways)])  56.8 us
    all_gather x1, waiting for transfers between devices, per_device(): slabs_got = lax.all_gather(flat_slabs, 'ao', axis=0, tiled=True)  36.7 us
    ppermute x1, waiting for transfers between devices, per_device(): lax.ppermute(going_down, 'aux', [(d, (d - 1) % ways) for d in range(ways)])  25.9 us
    dot_general x1, matrix products, per_device(): jnp.dot(rows_whole, vir_coef, preferred_element_type=jnp.float32)  15.2 us
    unnamed x1, blocking collectives  9.49 us
    all_gather x1, blocking collectives, per_device(): occ_all = lax.all_gather(occ_coef, 'ao', axis=0, tiled=True)  8.6 us
    all_gather x1, blocking collectives, per_device(): lax.all_gather(pairs, 'ao', axis=0, tiled=True)  8.6 us
  transfers between devices with their start and end apart: 5, of which 5 were waited for; matrix products, arithmetic and copies ran while one was open for 1% of the time, Pallas kernels for 0%

profile of v1, /device:TPU:0, one launch (start us, length us, event | category | flops | bytes accessed | tf_op | source)
XLA Modules:
  0.0 279.1 jit_solution(15695172732687264339)
XLA Ops:
  6.5 0.0 all-gather.3.cloned.1.call-start
  7.2 0.7 slice_bitcast_fusion.1
  7.9 1.3 dynamic-slice
  9.8 0.7 dynamic-update-slice.1
  10.5 0.8 dynamic-update-slice
  11.3 9.5 %all-reduce.2 = (s32[80]{0:T(128)S(1)}, s32[8]{0:T(128)S(1)}) all-reduce(s32[80]{0:T(128)S(1)} %dynamic-update-slice, s32[8]{0:T(128)S(1)} %dynamic-update-slice.1), channel_id=1, replica_groups=mesh['ao'=8,'aux'=4] {'ao'}, use_global_device_ids=true, to_apply=%add | all-reduce | flops 88 | bytes 704
  20.8 0.2 select_reduce_fusion.1
  21.0 8.6 %all_gather.15 = bf16[80,8,128]{2,1,0:T(8,128)(2,1)S(1)} all-gather(bf16[10,8,128]{2,1,0:T(8,128)(2,1)} %param.10), channel_id=1, replica_groups=mesh['ao'=8,'aux'=4] {'ao'}, dimensions={0}, use_global_device_ids=true | all-gather | bytes 184320 | tf_op jit(solution)/shard_map/all_gather | solution.py:25
  29.6 0.6 gather_fusion
  30.2 0.0 copy-start
  30.2 7.2 %fusion.4 = bf16[6,512,128]{2,1,0:T(8,128)(2,1)} fusion(bf16[6,64,128,128]{3,2,1,0:T(8,128)(2,1)} %param.6, pred[6]{0:T(512)(128)(4,1)S(1)} %iota_compare_fusion.2, bf16[6,8,128]{2,1,0:T(8,128)(2,1)S(1)} %gather_fusion), kind=kOutput, calls=%fused_computation.6 | convolution fusion | flops 101449728 | bytes 13381638 | tf_op jit(solution)/shard_map/sim,spmn->spin/dot_general | solution.py:31
  37.4 0.0 all-gather.3.cloned.1.call-update
  37.4 0.0 reduce-scatter.2.cloned.1.call-start
  37.5 0.0 copy-done
  37.5 8.6 %all-gather = s32[8,6,2]{1,2,0:T(2,128)S(1)} all-gather(s32[1,6,2]{1,2,0:T(2,128)S(1)} %bitcast.37), channel_id=1, replica_groups=mesh['ao'=8,'aux'=4] {'ao'}, dimensions={0}, use_global_device_ids=true | all-gather | bytes 432 | tf_op jit(solution)/shard_map/all_gather | solution.py:21
  46.1 0.1 reshape.75
  46.2 0.1 iota_compare_fusion.1
  46.2 0.1 lt.78
  46.3 0.2 select_reduce_fusion
  46.6 36.7 %all-gather.3.cloned.1.call-done = bf16[48,512,128]{2,1,0:T(8,128)(2,1)} async-done(((bf16[6,512,128]{2,1,0:T(8,128)(2,1)}), bf16[48,512,128]{2,1,0:T(8,128)(2,1)}) %all-gather.3.cloned.1.call-update) | async-done | bytes 6291472 | tf_op jit(solution)/shard_map/all_gather | solution.py:40
  83.2 6.4 %convert_bitcast_fusion = bf16[512,10,128]{2,1,0:T(8,128)(2,1)S(1)} fusion(bf16[48,512,128]{2,1,0:T(8,128)(2,1)} %all-gather.3.cloned.1.call-done, s32[48]{0:T(128)S(1)} %and_select_fusion, pred[48]{0:T(512)(128)(4,1)S(1)} %compare_and_fusion), kind=kOutput, calls=%fused_computation.4 | convolution fusion | flops 63570880 | bytes 7602416 | tf_op jit(solution)/shard_map/lt,tqm->qlm/dot_general | solution.py:44
  89.7 1.5 copy.17
  91.2 1.5 collective-permute-start
  92.7 2.3 collective-permute-start.1
  95.1 29.7 %collective-permute-done = bf16[512,1280]{0,1:T(8,128)(2,1)S(1)} collective-permute-done((bf16[512,1280]{0,1:T(8,128)(2,1)S(1)}, bf16[512,1280]{0,1:T(8,128)(2,1)S(1)}, u32[]{:S(2)}, u32[]{:S(2)}) %collective-permute-start) | collective-permute-done | bytes 1310752 | tf_op jit(solution)/shard_map/ppermute | solution.py:53
  124.8 0.0 collective-permute-start.2
  124.8 0.0 slice-start
  124.8 0.6 broadcast_in_dim.38
  125.4 0.2 constant_dynamic-update-slice_fusion.3
  125.6 0.0 slice-start.1
  125.6 0.2 constant_dynamic-update-slice_fusion.2
  125.8 25.9 %collective-permute-done.1 = bf16[512,1280]{0,1:T(8,128)(2,1)} collective-permute-done((bf16[512,1280]{0,1:T(8,128)(2,1)S(1)}, bf16[512,1280]{0,1:T(8,128)(2,1)}, u32[]{:S(2)}, u32[]{:S(2)}) %collective-permute-start.1) | collective-permute-done | bytes 1310752 | tf_op jit(solution)/shard_map/ppermute | solution.py:56
  151.7 1.5 constant_dynamic-update-slice_fusion.1
  153.2 27.1 %collective-permute-done.2 = bf16[512,1280]{0,1:T(8,128)(2,1)} collective-permute-done((bf16[512,1280]{0,1:T(8,128)(2,1)S(1)}, bf16[512,1280]{0,1:T(8,128)(2,1)}, u32[]{:S(2)}, u32[]{:S(2)}) %collective-permute-start.2) | collective-permute-done | bytes 1310752 | tf_op jit(solution)/shard_map/ppermute | solution.py:53
  180.3 1.5 constant_dynamic-update-slice_fusion
  181.8 0.0 slice-done
  181.8 0.0 slice-done.1
  181.8 15.2 %convolution_convert_fusion = bf16[2048,2304]{1,0:T(8,128)(2,1)} fusion(bf16[2048,1280]{0,1:T(8,128)(2,1)S(1)} %constant_dynamic-update-slice_fusion, bf16[1280,2304]{1,0:T(8,128)(2,1)S(1)} %bitcast.39), kind=kOutput, calls=%fused_computation.1 | convolution fusion | flops 12084314112 | bytes 20578304 | tf_op jit(solution)/shard_map/dot_general | solution.py:63
  197.1 0.0 reduce-scatter.2.cloned.1.call-update
  197.1 75.1 %reduce-scatter.2.cloned.1.call-done = bf16[256,2304]{1,0:T(8,128)(2,1)} async-done(((bf16[2048,2304]{1,0:T(8,128)(2,1)}), bf16[256,2304]{1,0:T(8,128)(2,1)}) %reduce-scatter.2.cloned.1.call-update) | async-done | bytes 1179664 | tf_op jit(solution)/shard_map/reduce_scatter | solution.py:62
  (10 shorter events, 0.1 us)
Async XLA Ops:
  6.5 76.7 %all-gather.3.cloned.1.call-start = ((), (), s32[]{:S(2)}) async-start(), calls=%async_computation.1 | async-start | bytes 7077888 | tf_op jit(solution)/shard_map/all_gather | solution.py:40
  30.2 7.3 %copy-start = (s32[6,2]{0,1:T(2,128)S(1)}, s32[6,2]{0,1:T(2,128)}, u32[]{:S(2)}) copy-start(s32[6,2]{0,1:T(2,128)} %param.7) | copy-start | bytes 148
  37.4 234.8 %reduce-scatter.2.cloned.1.call-start = ((), (), s32[]{:S(2)}) async-start(), calls=%async_computation.2 | async-start | bytes 10616832 | tf_op jit(solution)/shard_map/reduce_scatter | solution.py:62
  91.2 33.5 %collective-permute-start = (bf16[512,1280]{0,1:T(8,128)(2,1)S(1)}, bf16[512,1280]{0,1:T(8,128)(2,1)S(1)}, u32[]{:S(2)}, u32[]{:S(2)}) collective-permute-start(bf16[512,1280]{0,1:T(8,128)(2,1)S(1)} %bitcast.34), channel_id=1, source_target_pairs={{0,1},{1,2},{2,3},{3,0},{4,5},{5,6},{6,7},{7,4},{8,9},{9,10},{10,1... | collective-permute-start | bytes 3932168 | tf_op jit(solution)/shard_map/ppermute | solution.py:53
  92.7 58.9 %collective-permute-start.1 = (bf16[512,1280]{0,1:T(8,128)(2,1)S(1)}, bf16[512,1280]{0,1:T(8,128)(2,1)}, u32[]{:S(2)}, u32[]{:S(2)}) collective-permute-start(bf16[512,1280]{0,1:T(8,128)(2,1)S(1)} %bitcast.35), channel_id=1, source_target_pairs={{0,3},{1,0},{2,1},{3,2},{4,7},{5,4},{6,5},{7,6},{8,11},{9,8},{10,9... | collective-permute-start | bytes 3932168 | tf_op jit(solution)/shard_map/ppermute | solution.py:56
  124.8 55.6 %collective-permute-start.2 = (bf16[512,1280]{0,1:T(8,128)(2,1)S(1)}, bf16[512,1280]{0,1:T(8,128)(2,1)}, u32[]{:S(2)}, u32[]{:S(2)}) collective-permute-start(bf16[512,1280]{0,1:T(8,128)(2,1)S(1)} %collective-permute-done), channel_id=1, source_target_pairs={{0,1},{1,2},{2,3},{3,0},{4,5},{5,6},{6,7},{7,4},{8,9},{9,10},{10,1... | collective-permute-start | bytes 3932168 | tf_op jit(solution)/shard_map/ppermute | solution.py:53
  124.8 57.1 %slice-start = ((s8[5898240]{0:T(1024)(128)(4,1)}), s8[4194304]{0:T(1024)(128)(4,1)S(1)}, s32[]{:S(2)}) async-start(s8[5898240]{0:T(1024)(128)(4,1)} %bitcast.38), calls=%async_computation.3 | async-start | bytes 8388608
  125.6 56.2 %slice-start.1 = ((s8[5898240]{0:T(1024)(128)(4,1)}), s8[1703936]{0:T(1024)(128)(4,1)S(1)}, s32[]{:S(2)}) async-start(s8[5898240]{0:T(1024)(128)(4,1)} %bitcast.38), calls=%async_computation.4 | async-start | bytes 3407872
Sparse Core Ops, SparseCore 0:
  37.5 45.6 all-gather.2
  197.2 74.9 reduce-scatter.1
